TPU v7x, 32 devices: a whole 2x2x4 slice. The times are simulated.
32 devices in a mesh: seqa: 8 (over z, x), seqb: 4 (over y, core).
Axes of the slice: x: 2, y: 2, z: 4, core: 2. Of those that a mesh axis runs over, the one named last changes fastest.
Arguments:
- queries: bfloat16 [16384, 4096], P(('seqa', 'seqb')), may hold values from -60 to 60
- keys: bfloat16 [16384, 1024], P(('seqa', 'seqb')), may hold values from -8 to 8
- values: bfloat16 [16384, 1024], P(('seqa', 'seqb')), may hold values from -6 to 6
- doc_start: int32 [16384], P(('seqa', 'seqb')), may hold values from 0 to 16383, as said below
Outputs:
- attended: bfloat16 [16384, 4096], P(('seqa', 'seqb'))
Inputs may be any that keep to these rules, and one draw needn't show every extreme that they name: Never falling along the sequence, doc_start[i] <= i, the same value for all tokens of one document, and doc_start[0] = 0.
All inputs are finite; a program needn't handle non-finite values.
Results may differ from a plain program's by a relative error of at most 0.0038.
Values may be sent and summed in bfloat16 or wider, within the bound.
No kernel may reach another device: no remote copies, remote signals or barrier semaphores. Data moves between devices by JAX's collectives and lax.ppermute only.
A program may use at most 64 MiB of HBM per device.

v0:
```python
import math

import jax
import jax.numpy as jnp
from jax import lax
from jax.sharding import PartitionSpec as P

HEAD_SIZE = 128


def passed_along(block, axis, distance):
    devices = range(lax.axis_size(axis))
    route = [(i - distance, i) for i in devices if i - distance in devices]
    return lax.ppermute(block, axis, route)


def attend_block(
    block_of_queries, block_of_keys, block_of_values, query_place, key_place, starts, window_length
):
    score_scale = 1.0 / math.sqrt(block_of_queries.shape[-1])
    scores = (
        jnp.einsum(
            "tgd,kd->gtk", block_of_queries, block_of_keys, preferred_element_type=jnp.float32
        )
        * score_scale
    )
    visible = (
        (key_place[None, :] <= query_place[:, None])
        & (key_place[None, :] > query_place[:, None] - window_length)
        & (key_place[None, :] >= starts[:, None])
    )
    scores = jnp.where(visible[None], scores, jnp.float32(-1e30))
    row_top = jnp.max(scores, axis=-1, keepdims=True)
    exponent = jnp.where(visible[None], jnp.exp(scores - row_top), jnp.float32(0.0))
    row_sum = jnp.sum(exponent, axis=-1, keepdims=True)
    weights = exponent.astype(jnp.bfloat16)
    summed = jnp.einsum("gtk,kd->tgd", weights, block_of_values, preferred_element_type=jnp.float32)
    return summed / jnp.transpose(row_sum, (1, 0, 2))


def local(queries, keys, values, doc_start):
    shard_rows = queries.shape[0]
    head_width = HEAD_SIZE
    group_width = queries.shape[1] // keys.shape[1]
    kv_heads = keys.shape[1] // head_width
    key_value = (keys, values)
    first_back = passed_along((key_value[0], key_value[1]), ("seqa", "seqb"), 1)
    second_back = passed_along((key_value[0], key_value[1]), ("seqa", "seqb"), 2)
    key_all = jnp.concatenate([second_back[0], first_back[0], keys], axis=0)
    value_all = jnp.concatenate([second_back[1], first_back[1], values], axis=0)
    window_length = 2 * shard_rows
    rows_per_block = min(512, shard_rows)
    block_count = shard_rows // rows_per_block
    shard_start = lax.axis_index(("seqa", "seqb")) * shard_rows

    def one_step(step_index, output):
        kv_head = step_index // block_count
        offset = step_index % block_count * rows_per_block
        block_of_queries = lax.dynamic_slice(
            queries,
            (offset, kv_head * group_width * head_width),
            (rows_per_block, group_width * head_width),
        )
        block_of_queries = block_of_queries.reshape(rows_per_block, group_width, head_width)
        block_of_keys = lax.dynamic_slice(
            key_all, (offset, kv_head * head_width), (window_length + rows_per_block, head_width)
        )
        block_of_values = lax.dynamic_slice(
            value_all, (offset, kv_head * head_width), (window_length + rows_per_block, head_width)
        )
        query_place = shard_start + offset + jnp.arange(rows_per_block, dtype=jnp.int32)
        key_place = (
            shard_start
            - window_length
            + offset
            + jnp.arange(window_length + rows_per_block, dtype=jnp.int32)
        )
        attended_block = attend_block(
            block_of_queries,
            block_of_keys,
            block_of_values,
            query_place,
            key_place,
            doc_start,
            window_length,
        )
        attended_block = attended_block.reshape(rows_per_block, group_width * head_width).astype(
            jnp.bfloat16
        )
        return lax.dynamic_update_slice(
            output, attended_block, (offset, kv_head * group_width * head_width)
        )

    return lax.fori_loop(0, kv_heads * block_count, one_step, jnp.zeros_like(queries))


def solution(mesh):
    return jax.shard_map(
        local,
        mesh=mesh,
        in_specs=(
            P(("seqa", "seqb"), None),
            P(("seqa", "seqb"), None),
            P(("seqa", "seqb"), None),
            P(("seqa", "seqb")),
        ),
        out_specs=P(("seqa", "seqb"), None),
        check_vma=False,
    )
```

profile of v0, /device:TPU:8, one launch (start us, length us, event | category | flops | bytes accessed | tf_op | source)
XLA Modules:
  0.0 212.1 jit_solution(15962611218056392615)
XLA Ops:
  0.0 1.6 copy.12
  1.6 1.9 collective-permute-start.1
  3.5 3.4 %collective-permute-start = (bf16[512,1024]{0,1:T(8,128)(2,1)S(1)}, bf16[512,1024]{0,1:T(8,128)(2,1)}, u32[]{:S(2)}, u32[]{:S(2)}) collective-permute-start(bf16[512,1024]{0,1:T(8,128)(2,1)S(1)} %copy.12), channel_id=1, source_target_pairs={{0,2},{1,3},{2,4},{3,5},{4,6},{5,7},{6,8},{7,9},{8,10},{9,11},{10,... | collective-permute-start | bytes 3145736 | tf_op jit(solution)/shard_map/ppermute | solution.py:14
  7.0 3.3 %collective-permute-start.2 = (bf16[512,1024]{1,0:T(8,128)(2,1)}, bf16[512,1024]{1,0:T(8,128)(2,1)S(1)}, u32[]{:S(2)}, u32[]{:S(2)}) collective-permute-start(bf16[512,1024]{1,0:T(8,128)(2,1)} %param.7), channel_id=1, source_target_pairs={{0,2},{1,3},{2,4},{3,5},{4,6},{5,7},{6,8},{7,9},{8,10},{9,11},{10,... | collective-permute-start | bytes 3145736 | tf_op jit(solution)/shard_map/ppermute | solution.py:14
  10.3 3.0 %collective-permute-start.3 = (bf16[512,1024]{1,0:T(8,128)(2,1)}, bf16[512,1024]{1,0:T(8,128)(2,1)}, u32[]{:S(2)}, u32[]{:S(2)}) collective-permute-start(bf16[512,1024]{1,0:T(8,128)(2,1)} %param.7), channel_id=1, source_target_pairs={{0,1},{1,2},{2,3},{3,4},{4,5},{5,6},{6,7},{7,8},{8,9},{9,10},{10,1... | collective-permute-start | bytes 3145736 | tf_op jit(solution)/shard_map/ppermute | solution.py:14
  13.3 15.0 %collective-permute-done.1 = bf16[512,1024]{0,1:T(8,128)(2,1)} collective-permute-done((bf16[512,1024]{0,1:T(8,128)(2,1)S(1)}, bf16[512,1024]{0,1:T(8,128)(2,1)}, u32[]{:S(2)}, u32[]{:S(2)}) %collective-permute-start.1) | collective-permute-done | bytes 1048608 | tf_op jit(solution)/shard_map/ppermute | solution.py:14
  28.3 5.0 %collective-permute-done = bf16[512,1024]{0,1:T(8,128)(2,1)} collective-permute-done((bf16[512,1024]{0,1:T(8,128)(2,1)S(1)}, bf16[512,1024]{0,1:T(8,128)(2,1)}, u32[]{:S(2)}, u32[]{:S(2)}) %collective-permute-start) | collective-permute-done | bytes 1048608 | tf_op jit(solution)/shard_map/ppermute | solution.py:14
  33.4 3.0 %pad_maximum_fusion = bf16[1536,1024]{0,1:T(8,128)(2,1)} fusion(bf16[512,1024]{0,1:T(8,128)(2,1)S(1)} %copy.12, bf16[512,1024]{0,1:T(8,128)(2,1)} %collective-permute-done.1, bf16[512,1024]{0,1:T(8,128)(2,1)} %collective-permute-done), kind=kLoop, calls=%fused_computation.31 | loop fusion | flops 9437184 | bytes 6291456 | tf_op jit(solution)/shard_map/concatenate | solution.py:50
  36.4 19.4 %collective-permute-done.2 = bf16[512,1024]{1,0:T(8,128)(2,1)S(1)} collective-permute-done((bf16[512,1024]{1,0:T(8,128)(2,1)}, bf16[512,1024]{1,0:T(8,128)(2,1)S(1)}, u32[]{:S(2)}, u32[]{:S(2)}) %collective-permute-start.2) | collective-permute-done | bytes 1048608 | tf_op jit(solution)/shard_map/ppermute | solution.py:14
  55.7 20.1 %collective-permute-done.3 = bf16[512,1024]{1,0:T(8,128)(2,1)} collective-permute-done((bf16[512,1024]{1,0:T(8,128)(2,1)}, bf16[512,1024]{1,0:T(8,128)(2,1)}, u32[]{:S(2)}, u32[]{:S(2)}) %collective-permute-start.3) | collective-permute-done | bytes 1048608 | tf_op jit(solution)/shard_map/ppermute | solution.py:14
  75.8 2.9 %pad_maximum_fusion.1 = bf16[1536,1024]{1,0:T(8,128)(2,1)} fusion(bf16[512,1024]{1,0:T(8,128)(2,1)S(1)} %copy-done, bf16[512,1024]{1,0:T(8,128)(2,1)} %collective-permute-done.3, bf16[512,1024]{1,0:T(8,128)(2,1)S(1)} %collective-permute-done.2), kind=kLoop, calls=%fused_computation.32 | loop fusion | flops 9437184 | bytes 6291456 | tf_op jit(solution)/shard_map/concatenate | solution.py:49
  78.6 2.5 %broadcast_in_dim.82.clone = bf16[512,4096]{1,0:T(8,128)(2,1)} broadcast(bf16[]{:T(256)} %constant.186.clone.1), dimensions={} | broadcast | bytes 4194306 | tf_op jit(solution)/shard_map/broadcast_in_dim | solution.py:94
  81.2 131.0 %while.16 = (s32[]{:T(128)}, bf16[512,4096]{1,0:T(8,128)(2,1)}, bf16[1536,1024]{0,1:T(8,128)(2,1)}, s32[]{:T(128)}, s32[]{:T(128)}, /*index=5*/s32[512]{0:T(512)...) while((s32[]{:T(128)}, bf16[512,4096]{1,0:T(8,128)(2,1)}, ...), condition=%wide.region_3.4_spmd, body=%wide.region_0.3_spmd.sunk | while | flops 1633947648 | bytes 21010688 | solution.py:94
  81.2 1.1 constant_dynamic-slice_fusion.2
  82.3 0.2 copy.24
  82.5 1.2 compare_and_fusion.2
  83.6 8.9 %fusion.56 = (f32[4,512]{1,0:T(4,128)S(1)}, bf16[4,512,1536]{1,2,0:T(8,128)(2,1)}) fusion(pred[512,1536]{0,1:T(8,128)(4,1)S(1)} %compare_and_fusion.2, bf16[512,4,128]{0,2,1:T(8,128)(2,1)S(1)} %bitcast.61, bf16[1536,1024]{1,0:T(8,128)(2,1)} %get-tuple-element.346, s32[]{:T(128)S(6)} %select_n.95), kind=kOutput, calls=%fused_computation.33.clone.1 | convolution fusion | flops 824182272 | bytes 8790020 | tf_op jit(solution)/shard_map/while/body/eval_jaxpr/sub | solution.py:34
  92.6 3.9 %fusion.57 = bf16[512,4,128]{0,2,1:T(8,128)(2,1)S(1)} fusion(bf16[4,512,1536]{1,2,0:T(8,128)(2,1)} %get-tuple-element.310, f32[512,4]{0,1:T(4,128)S(1)} %bitcast.63, bf16[1536,1024]{0,1:T(8,128)(2,1)} %get-tuple-element.342, s32[]{:T(128)S(6)} %select_n.95), kind=kOutput, calls=%fused_computation.13.clone.1 | convolution fusion | flops 805830656 | bytes 7217156 | tf_op jit(solution)/shard_map/while/body/eval_jaxpr/gtk,kd->tgd/dot_general | solution.py:37
  96.5 0.2 copy.25
  96.7 0.8 constant_dynamic-update-slice_fusion.2
  97.6 1.1 constant_dynamic-slice_fusion.2
  98.6 0.2 copy.24
  98.9 1.2 compare_and_fusion.2
  100.0 8.9 %fusion.56 = (f32[4,512]{1,0:T(4,128)S(1)}, bf16[4,512,1536]{1,2,0:T(8,128)(2,1)}) fusion(pred[512,1536]{0,1:T(8,128)(4,1)S(1)} %compare_and_fusion.2, bf16[512,4,128]{0,2,1:T(8,128)(2,1)S(1)} %bitcast.61, bf16[1536,1024]{1,0:T(8,128)(2,1)} %get-tuple-element.346, s32[]{:T(128)S(6)} %select_n.95), kind=kOutput, calls=%fused_computation.33.clone.1 | convolution fusion | flops 824182272 | bytes 8790020 | tf_op jit(solution)/shard_map/while/body/eval_jaxpr/sub | solution.py:34
  108.9 3.9 %fusion.57 = bf16[512,4,128]{0,2,1:T(8,128)(2,1)S(1)} fusion(bf16[4,512,1536]{1,2,0:T(8,128)(2,1)} %get-tuple-element.310, f32[512,4]{0,1:T(4,128)S(1)} %bitcast.63, bf16[1536,1024]{0,1:T(8,128)(2,1)} %get-tuple-element.342, s32[]{:T(128)S(6)} %select_n.95), kind=kOutput, calls=%fused_computation.13.clone.1 | convolution fusion | flops 805830656 | bytes 7217156 | tf_op jit(solution)/shard_map/while/body/eval_jaxpr/gtk,kd->tgd/dot_general | solution.py:37
  113.1 0.8 constant_dynamic-update-slice_fusion.2
  113.9 1.1 constant_dynamic-slice_fusion.2
  115.0 0.2 copy.24
  115.2 1.2 compare_and_fusion.2
  116.4 8.9 %fusion.56 = (f32[4,512]{1,0:T(4,128)S(1)}, bf16[4,512,1536]{1,2,0:T(8,128)(2,1)}) fusion(pred[512,1536]{0,1:T(8,128)(4,1)S(1)} %compare_and_fusion.2, bf16[512,4,128]{0,2,1:T(8,128)(2,1)S(1)} %bitcast.61, bf16[1536,1024]{1,0:T(8,128)(2,1)} %get-tuple-element.346, s32[]{:T(128)S(6)} %select_n.95), kind=kOutput, calls=%fused_computation.33.clone.1 | convolution fusion | flops 824182272 | bytes 8790020 | tf_op jit(solution)/shard_map/while/body/eval_jaxpr/sub | solution.py:34
  125.3 3.9 %fusion.57 = bf16[512,4,128]{0,2,1:T(8,128)(2,1)S(1)} fusion(bf16[4,512,1536]{1,2,0:T(8,128)(2,1)} %get-tuple-element.310, f32[512,4]{0,1:T(4,128)S(1)} %bitcast.63, bf16[1536,1024]{0,1:T(8,128)(2,1)} %get-tuple-element.342, s32[]{:T(128)S(6)} %select_n.95), kind=kOutput, calls=%fused_computation.13.clone.1 | convolution fusion | flops 805830656 | bytes 7217156 | tf_op jit(solution)/shard_map/while/body/eval_jaxpr/gtk,kd->tgd/dot_general | solution.py:37
  129.2 0.2 copy.25
  129.5 0.8 constant_dynamic-update-slice_fusion.2
  130.3 1.1 constant_dynamic-slice_fusion.2
  131.4 0.2 copy.24
  131.6 1.2 compare_and_fusion.2
  132.8 8.9 %fusion.56 = (f32[4,512]{1,0:T(4,128)S(1)}, bf16[4,512,1536]{1,2,0:T(8,128)(2,1)}) fusion(pred[512,1536]{0,1:T(8,128)(4,1)S(1)} %compare_and_fusion.2, bf16[512,4,128]{0,2,1:T(8,128)(2,1)S(1)} %bitcast.61, bf16[1536,1024]{1,0:T(8,128)(2,1)} %get-tuple-element.346, s32[]{:T(128)S(6)} %select_n.95), kind=kOutput, calls=%fused_computation.33.clone.1 | convolution fusion | flops 824182272 | bytes 8790020 | tf_op jit(solution)/shard_map/while/body/eval_jaxpr/sub | solution.py:34
  141.7 3.9 %fusion.57 = bf16[512,4,128]{0,2,1:T(8,128)(2,1)S(1)} fusion(bf16[4,512,1536]{1,2,0:T(8,128)(2,1)} %get-tuple-element.310, f32[512,4]{0,1:T(4,128)S(1)} %bitcast.63, bf16[1536,1024]{0,1:T(8,128)(2,1)} %get-tuple-element.342, s32[]{:T(128)S(6)} %select_n.95), kind=kOutput, calls=%fused_computation.13.clone.1 | convolution fusion | flops 805830656 | bytes 7217156 | tf_op jit(solution)/shard_map/while/body/eval_jaxpr/gtk,kd->tgd/dot_general | solution.py:37
  145.6 0.2 copy.25
  145.8 0.8 constant_dynamic-update-slice_fusion.2
  146.7 1.1 constant_dynamic-slice_fusion.2
  148.0 1.2 compare_and_fusion.2
  149.1 8.9 %fusion.56 = (f32[4,512]{1,0:T(4,128)S(1)}, bf16[4,512,1536]{1,2,0:T(8,128)(2,1)}) fusion(pred[512,1536]{0,1:T(8,128)(4,1)S(1)} %compare_and_fusion.2, bf16[512,4,128]{0,2,1:T(8,128)(2,1)S(1)} %bitcast.61, bf16[1536,1024]{1,0:T(8,128)(2,1)} %get-tuple-element.346, s32[]{:T(128)S(6)} %select_n.95), kind=kOutput, calls=%fused_computation.33.clone.1 | convolution fusion | flops 824182272 | bytes 8790020 | tf_op jit(solution)/shard_map/while/body/eval_jaxpr/sub | solution.py:34
  158.1 3.9 %fusion.57 = bf16[512,4,128]{0,2,1:T(8,128)(2,1)S(1)} fusion(bf16[4,512,1536]{1,2,0:T(8,128)(2,1)} %get-tuple-element.310, f32[512,4]{0,1:T(4,128)S(1)} %bitcast.63, bf16[1536,1024]{0,1:T(8,128)(2,1)} %get-tuple-element.342, s32[]{:T(128)S(6)} %select_n.95), kind=kOutput, calls=%fused_computation.13.clone.1 | convolution fusion | flops 805830656 | bytes 7217156 | tf_op jit(solution)/shard_map/while/body/eval_jaxpr/gtk,kd->tgd/dot_general | solution.py:37
  162.2 0.8 constant_dynamic-update-slice_fusion.2
  163.0 1.1 constant_dynamic-slice_fusion.2
  164.1 0.2 copy.24
  164.3 1.2 compare_and_fusion.2
  165.5 8.9 %fusion.56 = (f32[4,512]{1,0:T(4,128)S(1)}, bf16[4,512,1536]{1,2,0:T(8,128)(2,1)}) fusion(pred[512,1536]{0,1:T(8,128)(4,1)S(1)} %compare_and_fusion.2, bf16[512,4,128]{0,2,1:T(8,128)(2,1)S(1)} %bitcast.61, bf16[1536,1024]{1,0:T(8,128)(2,1)} %get-tuple-element.346, s32[]{:T(128)S(6)} %select_n.95), kind=kOutput, calls=%fused_computation.33.clone.1 | convolution fusion | flops 824182272 | bytes 8790020 | tf_op jit(solution)/shard_map/while/body/eval_jaxpr/sub | solution.py:34
  174.4 3.9 %fusion.57 = bf16[512,4,128]{0,2,1:T(8,128)(2,1)S(1)} fusion(bf16[4,512,1536]{1,2,0:T(8,128)(2,1)} %get-tuple-element.310, f32[512,4]{0,1:T(4,128)S(1)} %bitcast.63, bf16[1536,1024]{0,1:T(8,128)(2,1)} %get-tuple-element.342, s32[]{:T(128)S(6)} %select_n.95), kind=kOutput, calls=%fused_computation.13.clone.1 | convolution fusion | flops 805830656 | bytes 7217156 | tf_op jit(solution)/shard_map/while/body/eval_jaxpr/gtk,kd->tgd/dot_general | solution.py:37
  178.4 0.2 copy.25
  178.6 0.8 constant_dynamic-update-slice_fusion.2
  179.4 1.1 constant_dynamic-slice_fusion.2
  180.5 0.2 copy.24
  180.7 1.2 compare_and_fusion.2
  181.9 8.9 %fusion.56 = (f32[4,512]{1,0:T(4,128)S(1)}, bf16[4,512,1536]{1,2,0:T(8,128)(2,1)}) fusion(pred[512,1536]{0,1:T(8,128)(4,1)S(1)} %compare_and_fusion.2, bf16[512,4,128]{0,2,1:T(8,128)(2,1)S(1)} %bitcast.61, bf16[1536,1024]{1,0:T(8,128)(2,1)} %get-tuple-element.346, s32[]{:T(128)S(6)} %select_n.95), kind=kOutput, calls=%fused_computation.33.clone.1 | convolution fusion | flops 824182272 | bytes 8790020 | tf_op jit(solution)/shard_map/while/body/eval_jaxpr/sub | solution.py:34
  190.8 3.9 %fusion.57 = bf16[512,4,128]{0,2,1:T(8,128)(2,1)S(1)} fusion(bf16[4,512,1536]{1,2,0:T(8,128)(2,1)} %get-tuple-element.310, f32[512,4]{0,1:T(4,128)S(1)} %bitcast.63, bf16[1536,1024]{0,1:T(8,128)(2,1)} %get-tuple-element.342, s32[]{:T(128)S(6)} %select_n.95), kind=kOutput, calls=%fused_computation.13.clone.1 | convolution fusion | flops 805830656 | bytes 7217156 | tf_op jit(solution)/shard_map/while/body/eval_jaxpr/gtk,kd->tgd/dot_general | solution.py:37
  194.7 0.2 copy.25
  194.9 0.8 constant_dynamic-update-slice_fusion.2
  195.8 1.1 constant_dynamic-slice_fusion.2
  197.1 1.2 compare_and_fusion.2
  198.2 8.9 %fusion.56 = (f32[4,512]{1,0:T(4,128)S(1)}, bf16[4,512,1536]{1,2,0:T(8,128)(2,1)}) fusion(pred[512,1536]{0,1:T(8,128)(4,1)S(1)} %compare_and_fusion.2, bf16[512,4,128]{0,2,1:T(8,128)(2,1)S(1)} %bitcast.61, bf16[1536,1024]{1,0:T(8,128)(2,1)} %get-tuple-element.346, s32[]{:T(128)S(6)} %select_n.95), kind=kOutput, calls=%fused_computation.33.clone.1 | convolution fusion | flops 824182272 | bytes 8790020 | tf_op jit(solution)/shard_map/while/body/eval_jaxpr/sub | solution.py:34
  207.2 3.9 %fusion.57 = bf16[512,4,128]{0,2,1:T(8,128)(2,1)S(1)} fusion(bf16[4,512,1536]{1,2,0:T(8,128)(2,1)} %get-tuple-element.310, f32[512,4]{0,1:T(4,128)S(1)} %bitcast.63, bf16[1536,1024]{0,1:T(8,128)(2,1)} %get-tuple-element.342, s32[]{:T(128)S(6)} %select_n.95), kind=kOutput, calls=%fused_computation.13.clone.1 | convolution fusion | flops 805830656 | bytes 7217156 | tf_op jit(solution)/shard_map/while/body/eval_jaxpr/gtk,kd->tgd/dot_general | solution.py:37
  211.3 0.8 constant_dynamic-update-slice_fusion.2
  (25 shorter events, 1.1 us)
Async XLA Ops:
  0.0 75.8 %copy-start = (bf16[512,1024]{1,0:T(8,128)(2,1)S(1)}, bf16[512,1024]{1,0:T(8,128)(2,1)}, u32[]{:S(2)}) copy-start(bf16[512,1024]{1,0:T(8,128)(2,1)} %param.7) | copy-start | bytes 3145732
  1.6 26.8 %collective-permute-start.1 = (bf16[512,1024]{0,1:T(8,128)(2,1)S(1)}, bf16[512,1024]{0,1:T(8,128)(2,1)}, u32[]{:S(2)}, u32[]{:S(2)}) collective-permute-start(bf16[512,1024]{0,1:T(8,128)(2,1)S(1)} %copy.12), channel_id=1, source_target_pairs={{0,1},{1,2},{2,3},{3,4},{4,5},{5,6},{6,7},{7,8},{8,9},{9,10},{10,1... | collective-permute-start | bytes 3145736 | tf_op jit(solution)/shard_map/ppermute | solution.py:14
  3.5 29.8 %collective-permute-start = (bf16[512,1024]{0,1:T(8,128)(2,1)S(1)}, bf16[512,1024]{0,1:T(8,128)(2,1)}, u32[]{:S(2)}, u32[]{:S(2)}) collective-permute-start(bf16[512,1024]{0,1:T(8,128)(2,1)S(1)} %copy.12), channel_id=1, source_target_pairs={{0,2},{1,3},{2,4},{3,5},{4,6},{5,7},{6,8},{7,9},{8,10},{9,11},{10,... | collective-permute-start | bytes 3145736 | tf_op jit(solution)/shard_map/ppermute | solution.py:14
  7.0 48.8 %collective-permute-start.2 = (bf16[512,1024]{1,0:T(8,128)(2,1)}, bf16[512,1024]{1,0:T(8,128)(2,1)S(1)}, u32[]{:S(2)}, u32[]{:S(2)}) collective-permute-start(bf16[512,1024]{1,0:T(8,128)(2,1)} %param.7), channel_id=1, source_target_pairs={{0,2},{1,3},{2,4},{3,5},{4,6},{5,7},{6,8},{7,9},{8,10},{9,11},{10,... | collective-permute-start | bytes 3145736 | tf_op jit(solution)/shard_map/ppermute | solution.py:14
  10.3 65.5 %collective-permute-start.3 = (bf16[512,1024]{1,0:T(8,128)(2,1)}, bf16[512,1024]{1,0:T(8,128)(2,1)}, u32[]{:S(2)}, u32[]{:S(2)}) collective-permute-start(bf16[512,1024]{1,0:T(8,128)(2,1)} %param.7), channel_id=1, source_target_pairs={{0,1},{1,2},{2,3},{3,4},{4,5},{5,6},{6,7},{7,8},{8,9},{9,10},{10,1... | collective-permute-start | bytes 3145736 | tf_op jit(solution)/shard_map/ppermute | solution.py:14
  36.4 44.8 %copy-start.1 = (s32[512]{0:T(512)S(1)}, s32[512]{0:T(512)}, u32[]{:S(2)}) copy-start(s32[512]{0:T(512)} %param.9) | copy-start | bytes 6148
where the time goes:
time: 213 us; the launch traced here: 212 us
  matrix products  103 us (48%)
  waiting for transfers between devices  59.5 us (28%)
  local copies, waits for them, and re-layouts  22.8 us (11%)
  other arithmetic  15.2 us (7%)
  starting transfers between devices  11.7 us (5%)
    sub x8, matrix products, attend_block(): scores - row_top  71.3 us
    ppermute x4, waiting for transfers between devices, passed_along(): return lax.ppermute(block, axis, route)  59.5 us
    dot_general x8, matrix products, attend_block(): jnp.einsum('gtk,kd->tgd', weights, block_of_values, preferred_element_typ...  31.4 us
    ppermute x4, starting transfers between devices, passed_along(): return lax.ppermute(block, axis, route)  11.7 us
    dynamic_slice x16, local copies, waits for them, and re-layouts, one_step(): lax.dynamic_slice(queries, (offset, kv_head * group_width * head_width),...  10.3 us
    and x8, other arithmetic, attend_block(): (key_place[None, :] <= query_place[:, None]) & (key_place[None, :] > quer...  9.27 us
    dynamic_update_slice x16, local copies, waits for them, and re-layouts, one_step(): lax.dynamic_update_slice(output, attended_block, (offset, kv_head * group...  8.37 us
  transfers between devices with their start and end apart: 4, of which 4 were waited for; matrix products, arithmetic and copies ran while one was open for 1% of the time, Pallas kernels for 0%

commit v1 on v0

v1 whole, which is shorter than its diff:
```python
import functools
import math

import jax
import jax.numpy as jnp
from jax import lax
from jax.experimental import pallas as pl
from jax.experimental.pallas import tpu as pltpu
from jax.sharding import PartitionSpec as P

HEAD_SIZE = 128
ROWS = 128
AXES = ("seqa", "seqb")
HIDDEN = -1e30


def attend_kernel(place, starts, q, k2, v2, k1, v1, k0, v0, *rest):
    out, bias = rest[-2], rest[-1]
    shard = q.shape[0]
    head = k0.shape[1]
    group = q.shape[1] // head
    window = 2 * shard
    width = window + ROWS
    blocks = shard // ROWS
    factor = math.log2(math.e) / math.sqrt(head)

    @pl.when(pl.program_id(0) == 0)
    def _():
        for b in range(blocks):
            row = lax.broadcasted_iota(jnp.int32, (ROWS, width), 0) + b * ROWS
            col = lax.broadcasted_iota(jnp.int32, (ROWS, width), 1) + (b * ROWS - window)
            start = starts[b * ROWS : (b + 1) * ROWS, :] - place[0]
            visible = (col <= row) & (col > row - window) & (col >= start)
            bias[b] = jnp.where(visible, jnp.float32(0.0), jnp.float32(HIDDEN))

    ones = jnp.ones((width, head), jnp.bfloat16)
    for b in range(blocks):
        lo, hi = b * ROWS, (b + 1) * ROWS
        keys = jnp.concatenate([k2[lo:, :], k1[...], k0[:hi, :]], axis=0)
        vals = jnp.concatenate([v2[lo:, :], v1[...], v0[:hi, :]], axis=0)
        vals = jnp.concatenate([vals, ones], axis=1)
        for g in range(group):
            qg = q[lo:hi, g * head : (g + 1) * head]
            s = lax.dot_general(qg, keys, (((1,), (1,)), ((), ())), preferred_element_type=jnp.float32)
            s = s + bias[b]
            top = jnp.max(s, axis=-1, keepdims=True)
            w = jnp.exp2((s - top) * factor).astype(jnp.bfloat16)
            o = lax.dot_general(w, vals, (((1,), (0,)), ((), ())), preferred_element_type=jnp.float32)
            out[lo:hi, g * head : (g + 1) * head] = (o[:, :head] / o[:, head:]).astype(jnp.bfloat16)


def attend(place, starts, queries, second, first, keys, values, partial, h0, n):
    shard = queries.shape[0]
    group = queries.shape[1] // keys.shape[1]
    head = HEAD_SIZE
    kv = lambda f: pl.BlockSpec((shard, head), f)
    wide = pl.BlockSpec((shard, group * head), lambda j: (0, h0 + j))
    in_specs = [
        pl.BlockSpec(memory_space=pltpu.SMEM),
        pl.BlockSpec((shard, 1), lambda j: (0, 0)),
        wide,
        kv(lambda j: (0, j)),
        kv(lambda j: (0, n + j)),
        kv(lambda j: (0, j)),
        kv(lambda j: (0, n + j)),
        kv(lambda j: (0, h0 + j)),
        kv(lambda j: (0, h0 + j)),
    ]
    args = [place, starts, queries, second, second, first, first, keys, values]
    aliases = {}
    if partial is not None:
        in_specs.append(pl.BlockSpec(memory_space=pl.ANY))
        aliases = {len(args): 0}
        args.append(partial)
    width = 2 * shard + ROWS
    return pl.pallas_call(
        attend_kernel,
        grid=(n,),
        in_specs=in_specs,
        out_specs=wide,
        out_shape=jax.ShapeDtypeStruct(queries.shape, queries.dtype),
        scratch_shapes=[pltpu.VMEM((shard // ROWS, ROWS, width), jnp.float32)],
        input_output_aliases=aliases,
        compiler_params=pltpu.CompilerParams(dimension_semantics=("arbitrary",)),
        cost_estimate=pl.CostEstimate(
            flops=n * group * shard * width * head * 6,
            transcendentals=n * group * shard * width,
            bytes_accessed=n * head * shard * 2 * (2 * group + 6),
        ),
        name="attend",
    )(*args)


def chunk_sizes(heads):
    sizes = []
    left = heads
    while left:
        n = min(left, 2 if left > 2 else 1)
        sizes.append(n)
        left -= n
    return sizes


def local(queries, keys, values, doc_start):
    shard = queries.shape[0]
    head = HEAD_SIZE
    heads = keys.shape[1] // head
    count = lax.axis_size(AXES)
    me = lax.axis_index(AXES)
    ahead = [(i, i + 2) for i in range(count - 2)]
    swap = [(i, i ^ 1) for i in range(count)]
    place = (me * shard).astype(jnp.int32).reshape(1)
    starts = doc_start.reshape(shard, 1)
    even = me % 2 == 0

    sent, spans, h0 = [], [], 0
    for n in chunk_sizes(heads):
        cols = slice(h0 * head, (h0 + n) * head)
        sent.append(jnp.concatenate([keys[:, cols], values[:, cols]], axis=1))
        spans.append((h0, n))
        h0 += n
    out = None
    for chunk, (h0, n) in zip(sent, spans):
        second = lax.ppermute(chunk, AXES, ahead)
        if out is not None:
            second, out = lax.optimization_barrier((second, out))
        first = lax.ppermute(jnp.where(even, chunk, second), AXES, swap)
        out = attend(place, starts, queries, second, first, keys, values, out, h0, n)
    return out


def solution(mesh):
    return jax.shard_map(
        local,
        mesh=mesh,
        in_specs=(P(AXES, None), P(AXES, None), P(AXES, None), P(AXES)),
        out_specs=P(AXES, None),
        check_vma=False,
    )
```

time: 213 us -> 92.2 us (0.43)
  matrix products: 103 us -> 0 us
  Pallas kernels: 0 us -> 43.4 us
  waiting for transfers between devices: 59.5 us -> 28.6 us
  local copies, waits for them, and re-layouts: 22.8 us -> 6.44 us
  other arithmetic: 15.2 us -> 0.69 us
    sub x8 -> x0, matrix products: 71.3 us -> none  [attend_block(): scores - row_top]
    pallas_call x0 -> x5, Pallas kernels: none -> 43.4 us  [attend(): pl.pallas_call(attend_kernel, grid=(n,), in_specs=in_specs, out_specs=wid...]
    dot_general x8 -> x0, matrix products: 31.4 us -> none  [attend_block(): jnp.einsum('gtk,kd->tgd', weights, block_of_values, preferred_element_typ...]
    ppermute x4 -> x10, waiting for transfers between devices: 59.5 us -> 28.6 us  [the longest x5 27.1 us: local(): second = lax.ppermute(chunk, AXES, ahead)]
    dynamic_slice x16 -> x0, local copies, waits for them, and re-layouts: 10.3 us -> none  [one_step(): lax.dynamic_slice(queries, (offset, kv_head * group_width * head_width),...]
    and x8 -> x0, other arithmetic: 9.27 us -> none  [attend_block(): (key_place[None, :] <= query_place[:, None]) & (key_place[None, :] > quer...]
    dynamic_update_slice x16 -> x0, local copies, waits for them, and re-layouts: 8.37 us -> none  [one_step(): lax.dynamic_update_slice(output, attended_block, (offset, kv_head * group...]
    concatenate x2 -> x5, other arithmetic: 5.85 us -> 0.17 us  [local(): sent.append(jnp.concatenate([keys[:, cols], values[:, cols]], axis=1))]
  transfers between devices with their start and end apart: 4 -> 10, of which waited for: 4 -> 5; matrix products, arithmetic and copies ran while one was open for 1% -> 2% of each run, Pallas kernels for 0% -> 41%
where the time goes in v1:
time: 92.2 us; the launch traced here: 91.5 us
  Pallas kernels  43.4 us (47%)
  waiting for transfers between devices  28.6 us (31%)
  starting transfers between devices  12.1 us (13%)
  local copies, waits for them, and re-layouts  6.44 us (7%)
    pallas_call x5, Pallas kernels, attend(): pl.pallas_call(attend_kernel, grid=(n,), in_specs=in_specs, out_specs=wid...  43.4 us
    ppermute x5, waiting for transfers between devices, local(): second = lax.ppermute(chunk, AXES, ahead)  27.1 us
    ppermute x5, starting transfers between devices, local(): second = lax.ppermute(chunk, AXES, ahead)  11.3 us
    unnamed x20, local copies, waits for them, and re-layouts  2.95 us
    slice x2, local copies, waits for them, and re-layouts, local(): sent.append(jnp.concatenate([keys[:, cols], values[:, cols]], axis=1))  2.63 us
  transfers between devices with their start and end apart: 10, of which 5 were waited for; matrix products, arithmetic and copies ran while one was open for 2% of the time, Pallas kernels for 41%

profile of v1, /device:TPU:8, one launch (start us, length us, event | category | flops | bytes accessed | tf_op | source)
XLA Modules:
  0.0 91.5 jit_solution(2476004751232518918)
XLA Ops:
  0.0 0.0 copy-start.9
  0.0 1.5 %fusion = (bf16[512,256]{1,0:T(8,128)(2,1)S(1)}, bf16[512,256]{1,0:T(8,128)(2,1)S(1)}, bf16[512,256]{1,0:T(8,128)(2,1)S(1)}, bf16[512,256]{1,0:T(8,128)(2,1)S(1)...) fusion(bf16[512,1024]{1,0:T(8,128)(2,1)} %k0.9, bf16[512,1024]{1,0:T(8,128)(2,1)} %v0.9), kind=kLoop, calls=%fused_computation.10 | loop fusion | bytes 3145728 | tf_op jit(solution)/shard_map/slice | solution.py:119
  1.5 3.4 %collective-permute-start.4 = (bf16[512,512]{1,0:T(8,128)(2,1)S(1)}, bf16[512,512]{1,0:T(8,128)(2,1)S(1)}, u32[]{:S(2)}, u32[]{:S(2)}) collective-permute-start(bf16[512,512]{1,0:T(8,128)(2,1)S(1)} %pad_maximum_fusion.2), channel_id=1, source_target_pairs={{0,2},{1,3},{2,4},{3,5},{4,6},{5,7},{6,8},{7,9},{8,10},{9,11},{10,... | collective-permute-start | bytes 1572872 | tf_op jit(solution)/shard_map/ppermute | solution.py:124
  5.0 13.9 %collective-permute-done.4.k2.v2 = bf16[512,512]{1,0:T(8,128)(2,1)S(1)} collective-permute-done((bf16[512,512]{1,0:T(8,128)(2,1)S(1)}, bf16[512,512]{1,0:T(8,128)(2,1)S(1)}, u32[]{:S(2)}, u32[]{:S(2)}) %collective-permute-start.4) | collective-permute-done | bytes 524320 | tf_op jit(solution)/shard_map/ppermute | solution.py:124
  18.9 0.0 copy-start.8
  18.9 0.1 broadcast_select_fusion.2
  19.0 0.1 collective-permute-start.5
  19.1 1.9 %collective-permute-start.3 = (bf16[512,512]{1,0:T(8,128)(2,1)S(1)}, bf16[512,512]{1,0:T(8,128)(2,1)S(1)}, u32[]{:S(2)}, u32[]{:S(2)}) collective-permute-start(bf16[512,512]{1,0:T(8,128)(2,1)S(1)} %pad_maximum_fusion.1), channel_id=1, source_target_pairs={{0,2},{1,3},{2,4},{3,5},{4,6},{5,7},{6,8},{7,9},{8,10},{9,11},{10,... | collective-permute-start | bytes 1572872 | tf_op jit(solution)/shard_map/ppermute | solution.py:124
  21.1 0.0 copy-done.9
  21.1 0.9 copy.13.starts
  21.9 0.0 collective-permute-done.5.k1.v1
  21.9 0.0 copy-done.8
  21.9 10.5 %attend.5.rest_0_ = bf16[512,4096]{1,0:T(8,128)(2,1)} custom-call(s32[1]{0:T(128)} %bitcast.place, s32[512,1]{1,0:T(8,128)} %copy.13.starts, bf16[512,4096]{1,0:T(8,128)(2,1)} %q.9, bf16[512,512]{1,0:T(8,128)(2,1)} %copy-done.8, bf16[512,512]{1,0:T(8,128)(2,1)} %copy-done.8, bf16[512,512]{1,0:T(8,128)(2,1)} %collective-permute-done.5.k1.v1, ...), custom_call_target="tpu_custom_call" | custom-call | flops 3623878656 | bytes 3670016 | tf_op jit(solution)/shard_map/attend/pallas_call | solution.py:76
  32.5 4.7 %collective-permute-done.3.k2.v2 = bf16[512,512]{1,0:T(8,128)(2,1)S(1)} collective-permute-done((bf16[512,512]{1,0:T(8,128)(2,1)S(1)}, bf16[512,512]{1,0:T(8,128)(2,1)S(1)}, u32[]{:S(2)}, u32[]{:S(2)}) %collective-permute-start.3) | collective-permute-done | bytes 524320 | tf_op jit(solution)/shard_map/ppermute | solution.py:124
  37.1 0.0 copy-start.1
  37.2 0.1 broadcast_select_fusion.1
  37.3 0.1 collective-permute-start.6
  37.4 1.9 %collective-permute-start.2 = (bf16[512,512]{1,0:T(8,128)(2,1)S(1)}, bf16[512,512]{1,0:T(8,128)(2,1)S(1)}, u32[]{:S(2)}, u32[]{:S(2)}) collective-permute-start(bf16[512,512]{1,0:T(8,128)(2,1)S(1)} %pad_maximum_fusion), channel_id=1, source_target_pairs={{0,2},{1,3},{2,4},{3,5},{4,6},{5,7},{6,8},{7,9},{8,10},{9,11},{10,... | collective-permute-start | bytes 1572872 | tf_op jit(solution)/shard_map/ppermute | solution.py:124
  39.3 0.0 collective-permute-done.6.k1.v1
  39.3 0.0 copy-done.1
  39.3 0.0 copy-start.5
  39.4 0.8 copy-done.5
  40.1 10.3 %attend.6.rest_0_ = bf16[512,4096]{1,0:T(8,128)(2,1)} custom-call(s32[1]{0:T(128)} %bitcast.place, s32[512,1]{1,0:T(8,128)} %copy.13.starts, bf16[512,4096]{1,0:T(8,128)(2,1)} %q.9, bf16[512,512]{1,0:T(8,128)(2,1)} %copy-done.1, bf16[512,512]{1,0:T(8,128)(2,1)} %copy-done.1, bf16[512,512]{1,0:T(8,128)(2,1)} %copy-done.5, ...), custom_call_target="tpu_custom_call", output_to_operand_aliasing={{}: (9, {})} | custom-call | flops 3623878656 | bytes 3670016 | tf_op jit(solution)/shard_map/attend/pallas_call | solution.py:76
  50.5 4.9 %collective-permute-done.2.k2.v2 = bf16[512,512]{1,0:T(8,128)(2,1)S(1)} collective-permute-done((bf16[512,512]{1,0:T(8,128)(2,1)S(1)}, bf16[512,512]{1,0:T(8,128)(2,1)S(1)}, u32[]{:S(2)}, u32[]{:S(2)}) %collective-permute-start.2) | collective-permute-done | bytes 524320 | tf_op jit(solution)/shard_map/ppermute | solution.py:124
  55.4 0.0 copy-start
  55.4 0.1 broadcast_select_fusion
  55.5 0.1 collective-permute-start.7
  55.6 1.1 %fusion.2 = (bf16[512,128]{1,0:T(8,128)(2,1)S(1)}, bf16[512,128]{1,0:T(8,128)(2,1)S(1)}, bf16[512,128]{1,0:T(8,128)(2,1)S(1)}, bf16[512,128]{1,0:T(8,128)(2,1)S(1)}) fusion(bf16[512,1024]{1,0:T(8,128)(2,1)} %k0.9, bf16[512,1024]{1,0:T(8,128)(2,1)} %v0.9), kind=kLoop, calls=%fused_computation.12 | loop fusion | bytes 1048576 | tf_op jit(solution)/shard_map/slice | solution.py:119
  56.8 2.1 %collective-permute-start.1 = (bf16[512,256]{1,0:T(8,128)(2,1)S(1)}, bf16[512,256]{1,0:T(8,128)(2,1)S(1)}, u32[]{:S(2)}, u32[]{:S(2)}) collective-permute-start(bf16[512,256]{1,0:T(8,128)(2,1)S(1)} %pad_maximum_fusion.4), channel_id=1, source_target_pairs={{0,2},{1,3},{2,4},{3,5},{4,6},{5,7},{6,8},{7,9},{8,10},{9,11},{10,... | collective-permute-start | bytes 786440 | tf_op jit(solution)/shard_map/ppermute | solution.py:124
  58.9 0.0 collective-permute-done.7.k1.v1
  58.9 0.0 copy-done
  58.9 0.0 copy-start.4
  59.0 0.8 copy-done.4
  59.7 10.5 %attend.7.rest_0_ = bf16[512,4096]{1,0:T(8,128)(2,1)} custom-call(s32[1]{0:T(128)} %bitcast.place, s32[512,1]{1,0:T(8,128)} %copy.13.starts, bf16[512,4096]{1,0:T(8,128)(2,1)} %q.9, bf16[512,512]{1,0:T(8,128)(2,1)} %copy-done, bf16[512,512]{1,0:T(8,128)(2,1)} %copy-done, bf16[512,512]{1,0:T(8,128)(2,1)} %copy-done.4, ...), custom_call_target="tpu_custom_call", output_to_operand_aliasing={{}: (9, {})} | custom-call | flops 3623878656 | bytes 3670016 | tf_op jit(solution)/shard_map/attend/pallas_call | solution.py:76
  70.2 0.0 collective-permute-done.1.k2.v2
  70.2 0.0 copy-start.2
  70.2 0.1 broadcast_select_fusion.4
  70.3 0.6 collective-permute-start.8
  70.9 1.9 %collective-permute-start = (bf16[512,256]{1,0:T(8,128)(2,1)S(1)}, bf16[512,256]{1,0:T(8,128)(2,1)S(1)}, u32[]{:S(2)}, u32[]{:S(2)}) collective-permute-start(bf16[512,256]{1,0:T(8,128)(2,1)S(1)} %pad_maximum_fusion.3), channel_id=1, source_target_pairs={{0,2},{1,3},{2,4},{3,5},{4,6},{5,7},{6,8},{7,9},{8,10},{9,11},{10,... | collective-permute-start | bytes 786440 | tf_op jit(solution)/shard_map/ppermute | solution.py:124
  72.9 0.0 collective-permute-done.8.k1.v1
  72.9 0.0 copy-done.2
  72.9 0.0 copy-start.6
  72.9 0.7 copy-done.6
  73.6 6.0 %attend.8.rest_0_ = bf16[512,4096]{1,0:T(8,128)(2,1)} custom-call(s32[1]{0:T(128)} %bitcast.place, s32[512,1]{1,0:T(8,128)} %copy.13.starts, bf16[512,4096]{1,0:T(8,128)(2,1)} %q.9, bf16[512,256]{1,0:T(8,128)(2,1)} %copy-done.2, bf16[512,256]{1,0:T(8,128)(2,1)} %copy-done.2, bf16[512,256]{1,0:T(8,128)(2,1)} %copy-done.6, ...), custom_call_target="tpu_custom_call", output_to_operand_aliasing={{}: (9, {})} | custom-call | flops 1811939328 | bytes 1835008 | tf_op jit(solution)/shard_map/attend/pallas_call | solution.py:76
  79.6 3.5 %collective-permute-done.k2.v2 = bf16[512,256]{1,0:T(8,128)(2,1)S(1)} collective-permute-done((bf16[512,256]{1,0:T(8,128)(2,1)S(1)}, bf16[512,256]{1,0:T(8,128)(2,1)S(1)}, u32[]{:S(2)}, u32[]{:S(2)}) %collective-permute-start) | collective-permute-done | bytes 262176 | tf_op jit(solution)/shard_map/ppermute | solution.py:124
  83.1 0.0 copy-start.3
  83.1 0.1 broadcast_select_fusion.3
  83.2 0.1 collective-permute-start.9
  83.3 1.5 %collective-permute-done.9.k1.v1 = bf16[512,256]{1,0:T(8,128)(2,1)S(1)} collective-permute-done((bf16[512,256]{1,0:T(8,128)(2,1)S(1)}, bf16[512,256]{1,0:T(8,128)(2,1)S(1)}, u32[]{:S(2)}, u32[]{:S(2)}) %collective-permute-start.9) | collective-permute-done | bytes 262176 | tf_op jit(solution)/shard_map/ppermute | solution.py:127
  84.8 0.0 copy-done.3
  84.8 0.0 copy-start.7
  84.8 0.7 copy-done.7
  85.5 6.0 %attend.9 = bf16[512,4096]{1,0:T(8,128)(2,1)} custom-call(s32[1]{0:T(128)} %bitcast.place, s32[512,1]{1,0:T(8,128)} %copy.13.starts, bf16[512,4096]{1,0:T(8,128)(2,1)} %q.9, bf16[512,256]{1,0:T(8,128)(2,1)} %copy-done.3, bf16[512,256]{1,0:T(8,128)(2,1)} %copy-done.3, bf16[512,256]{1,0:T(8,128)(2,1)} %copy-done.7, ...), custom_call_target="tpu_custom_call", output_to_operand_aliasing={{}: (9, {})} | custom-call | flops 1811939328 | bytes 1835008 | tf_op jit(solution)/shard_map/attend/pallas_call | solution.py:76
  (5 shorter events, 0.2 us)
Async XLA Ops:
  0.0 21.1 %copy-start.9 = (s32[512]{0:T(512)S(1)}, s32[512]{0:T(512)}, u32[]{:S(2)}) copy-start(s32[512]{0:T(512)} %param.7) | copy-start | bytes 6148
  1.5 17.4 %collective-permute-start.4 = (bf16[512,512]{1,0:T(8,128)(2,1)S(1)}, bf16[512,512]{1,0:T(8,128)(2,1)S(1)}, u32[]{:S(2)}, u32[]{:S(2)}) collective-permute-start(bf16[512,512]{1,0:T(8,128)(2,1)S(1)} %pad_maximum_fusion.2), channel_id=1, source_target_pairs={{0,2},{1,3},{2,4},{3,5},{4,6},{5,7},{6,8},{7,9},{8,10},{9,11},{10,... | collective-permute-start | bytes 1572872 | tf_op jit(solution)/shard_map/ppermute | solution.py:124
  18.9 3.1 %copy-start.8 = (bf16[512,512]{1,0:T(8,128)(2,1)}, bf16[512,512]{1,0:T(8,128)(2,1)S(1)}, u32[]{:S(2)}) copy-start(bf16[512,512]{1,0:T(8,128)(2,1)S(1)} %collective-permute-done.4.k2.v2) | copy-start | bytes 1572868
  19.0 2.9 %collective-permute-start.5 = (bf16[512,512]{1,0:T(8,128)(2,1)S(1)}, bf16[512,512]{1,0:T(8,128)(2,1)}, u32[]{:S(2)}, u32[]{:S(2)}) collective-permute-start(bf16[512,512]{1,0:T(8,128)(2,1)S(1)} %broadcast_select_fusion.2), channel_id=1, source_target_pairs={{0,1},{1,0},{2,3},{3,2},{4,5},{5,4},{6,7},{7,6},{8,9},{9,8},{10,11... | collective-permute-start | bytes 1572872 | tf_op jit(solution)/shard_map/ppermute | solution.py:127
  19.1 18.0 %collective-permute-start.3 = (bf16[512,512]{1,0:T(8,128)(2,1)S(1)}, bf16[512,512]{1,0:T(8,128)(2,1)S(1)}, u32[]{:S(2)}, u32[]{:S(2)}) collective-permute-start(bf16[512,512]{1,0:T(8,128)(2,1)S(1)} %pad_maximum_fusion.1), channel_id=1, source_target_pairs={{0,2},{1,3},{2,4},{3,5},{4,6},{5,7},{6,8},{7,9},{8,10},{9,11},{10,... | collective-permute-start | bytes 1572872 | tf_op jit(solution)/shard_map/ppermute | solution.py:124
  37.1 2.2 %copy-start.1 = (bf16[512,512]{1,0:T(8,128)(2,1)}, bf16[512,512]{1,0:T(8,128)(2,1)S(1)}, u32[]{:S(2)}) copy-start(bf16[512,512]{1,0:T(8,128)(2,1)S(1)} %collective-permute-done.3.k2.v2) | copy-start | bytes 1572868
  37.3 2.1 %collective-permute-start.6 = (bf16[512,512]{1,0:T(8,128)(2,1)S(1)}, bf16[512,512]{1,0:T(8,128)(2,1)S(1)}, u32[]{:S(2)}, u32[]{:S(2)}) collective-permute-start(bf16[512,512]{1,0:T(8,128)(2,1)S(1)} %broadcast_select_fusion.1), channel_id=1, source_target_pairs={{0,1},{1,0},{2,3},{3,2},{4,5},{5,4},{6,7},{7,6},{8,9},{9,8},{10,11... | collective-permute-start | bytes 1572872 | tf_op jit(solution)/shard_map/ppermute | solution.py:127
  37.4 18.0 %collective-permute-start.2 = (bf16[512,512]{1,0:T(8,128)(2,1)S(1)}, bf16[512,512]{1,0:T(8,128)(2,1)S(1)}, u32[]{:S(2)}, u32[]{:S(2)}) collective-permute-start(bf16[512,512]{1,0:T(8,128)(2,1)S(1)} %pad_maximum_fusion), channel_id=1, source_target_pairs={{0,2},{1,3},{2,4},{3,5},{4,6},{5,7},{6,8},{7,9},{8,10},{9,11},{10,... | collective-permute-start | bytes 1572872 | tf_op jit(solution)/shard_map/ppermute | solution.py:124
  39.3 0.8 copy-start.5
  55.4 3.5 %copy-start = (bf16[512,512]{1,0:T(8,128)(2,1)}, bf16[512,512]{1,0:T(8,128)(2,1)S(1)}, u32[]{:S(2)}) copy-start(bf16[512,512]{1,0:T(8,128)(2,1)S(1)} %collective-permute-done.2.k2.v2) | copy-start | bytes 1572868
  55.5 3.4 %collective-permute-start.7 = (bf16[512,512]{1,0:T(8,128)(2,1)S(1)}, bf16[512,512]{1,0:T(8,128)(2,1)S(1)}, u32[]{:S(2)}, u32[]{:S(2)}) collective-permute-start(bf16[512,512]{1,0:T(8,128)(2,1)S(1)} %broadcast_select_fusion), channel_id=1, source_target_pairs={{0,1},{1,0},{2,3},{3,2},{4,5},{5,4},{6,7},{7,6},{8,9},{9,8},{10,11... | collective-permute-start | bytes 1572872 | tf_op jit(solution)/shard_map/ppermute | solution.py:127
  56.8 13.4 %collective-permute-start.1 = (bf16[512,256]{1,0:T(8,128)(2,1)S(1)}, bf16[512,256]{1,0:T(8,128)(2,1)S(1)}, u32[]{:S(2)}, u32[]{:S(2)}) collective-permute-start(bf16[512,256]{1,0:T(8,128)(2,1)S(1)} %pad_maximum_fusion.4), channel_id=1, source_target_pairs={{0,2},{1,3},{2,4},{3,5},{4,6},{5,7},{6,8},{7,9},{8,10},{9,11},{10,... | collective-permute-start | bytes 786440 | tf_op jit(solution)/shard_map/ppermute | solution.py:124
  58.9 0.8 copy-start.4
  70.2 2.6 %copy-start.2 = (bf16[512,256]{1,0:T(8,128)(2,1)}, bf16[512,256]{1,0:T(8,128)(2,1)S(1)}, u32[]{:S(2)}) copy-start(bf16[512,256]{1,0:T(8,128)(2,1)S(1)} %collective-permute-done.1.k2.v2) | copy-start | bytes 786436
  70.3 2.5 %collective-permute-start.8 = (bf16[512,256]{1,0:T(8,128)(2,1)S(1)}, bf16[512,256]{1,0:T(8,128)(2,1)S(1)}, u32[]{:S(2)}, u32[]{:S(2)}) collective-permute-start(bf16[512,256]{1,0:T(8,128)(2,1)S(1)} %broadcast_select_fusion.4), channel_id=1, source_target_pairs={{0,1},{1,0},{2,3},{3,2},{4,5},{5,4},{6,7},{7,6},{8,9},{9,8},{10,11... | collective-permute-start | bytes 786440 | tf_op jit(solution)/shard_map/ppermute | solution.py:127
  70.9 12.2 %collective-permute-start = (bf16[512,256]{1,0:T(8,128)(2,1)S(1)}, bf16[512,256]{1,0:T(8,128)(2,1)S(1)}, u32[]{:S(2)}, u32[]{:S(2)}) collective-permute-start(bf16[512,256]{1,0:T(8,128)(2,1)S(1)} %pad_maximum_fusion.3), channel_id=1, source_target_pairs={{0,2},{1,3},{2,4},{3,5},{4,6},{5,7},{6,8},{7,9},{8,10},{9,11},{10,... | collective-permute-start | bytes 786440 | tf_op jit(solution)/shard_map/ppermute | solution.py:124
  72.9 0.7 copy-start.6
  83.1 1.7 %copy-start.3 = (bf16[512,256]{1,0:T(8,128)(2,1)}, bf16[512,256]{1,0:T(8,128)(2,1)S(1)}, u32[]{:S(2)}) copy-start(bf16[512,256]{1,0:T(8,128)(2,1)S(1)} %collective-permute-done.k2.v2) | copy-start | bytes 786436
  83.2 1.6 %collective-permute-start.9 = (bf16[512,256]{1,0:T(8,128)(2,1)S(1)}, bf16[512,256]{1,0:T(8,128)(2,1)S(1)}, u32[]{:S(2)}, u32[]{:S(2)}) collective-permute-start(bf16[512,256]{1,0:T(8,128)(2,1)S(1)} %broadcast_select_fusion.3), channel_id=1, source_target_pairs={{0,1},{1,0},{2,3},{3,2},{4,5},{5,4},{6,7},{7,6},{8,9},{9,8},{10,11... | collective-permute-start | bytes 786440 | tf_op jit(solution)/shard_map/ppermute | solution.py:127
  84.8 0.7 copy-start.7

commit v2 on v1

--- a/solution.py
+++ b/solution.py
@@ -1,4 +1,3 @@
-import functools
 import math
 
 import jax
@@ -7,6 +6,7 @@
 from jax.experimental import pallas as pl
 from jax.experimental.pallas import tpu as pltpu
 from jax.sharding import PartitionSpec as P
+
 
 HEAD_SIZE = 128
 ROWS = 128
@@ -39,14 +39,18 @@
         keys = jnp.concatenate([k2[lo:, :], k1[...], k0[:hi, :]], axis=0)
         vals = jnp.concatenate([v2[lo:, :], v1[...], v0[:hi, :]], axis=0)
         vals = jnp.concatenate([vals, ones], axis=1)
+        qs = jnp.concatenate([q[lo:hi, g * head : (g + 1) * head] for g in range(group)], axis=0)
+        s = lax.dot_general(qs, keys, (((1,), (1,)), ((), ())), preferred_element_type=jnp.float32)
+        ws = []
         for g in range(group):
-            qg = q[lo:hi, g * head : (g + 1) * head]
-            s = lax.dot_general(qg, keys, (((1,), (1,)), ((), ())), preferred_element_type=jnp.float32)
-            s = s + bias[b]
-            top = jnp.max(s, axis=-1, keepdims=True)
-            w = jnp.exp2((s - top) * factor).astype(jnp.bfloat16)
-            o = lax.dot_general(w, vals, (((1,), (0,)), ((), ())), preferred_element_type=jnp.float32)
-            out[lo:hi, g * head : (g + 1) * head] = (o[:, :head] / o[:, head:]).astype(jnp.bfloat16)
+            sg = s[g * ROWS : (g + 1) * ROWS, :] + bias[b]
+            top = jnp.max(sg, axis=-1, keepdims=True)
+            ws.append(jnp.exp2((sg - top) * factor).astype(jnp.bfloat16))
+        w = jnp.concatenate(ws, axis=0)
+        o = lax.dot_general(w, vals, (((1,), (0,)), ((), ())), preferred_element_type=jnp.float32)
+        o = (o[:, :head] / o[:, head:]).astype(jnp.bfloat16)
+        for g in range(group):
+            out[lo:hi, g * head : (g + 1) * head] = o[g * ROWS : (g + 1) * ROWS, :]
 
 
 def attend(place, starts, queries, second, first, keys, values, partial, h0, n):
@@ -92,16 +96,15 @@
 
 
 def chunk_sizes(heads):
-    sizes = []
-    left = heads
+    sizes, left = [], heads
     while left:
-        n = min(left, 2 if left > 2 else 1)
+        n = max(1, -(-left * 3 // 8))
         sizes.append(n)
         left -= n
     return sizes
 
 
-def local(queries, keys, values, doc_start):
+def layer(queries, keys, values, doc_start):
     shard = queries.shape[0]
     head = HEAD_SIZE
     heads = keys.shape[1] // head
@@ -131,7 +134,7 @@
 
 def solution(mesh):
     return jax.shard_map(
-        local,
+        layer,
         mesh=mesh,
         in_specs=(P(AXES, None), P(AXES, None), P(AXES, None), P(AXES)),
         out_specs=P(AXES, None),

time: 92.2 us -> 90.8 us (0.985)
  the two profiles are of different devices: /device:TPU:8 before, /device:TPU:15 now
where the time goes in v2:
time: 90.8 us; the launch traced here: 90.3 us
  Pallas kernels  42.8 us (47%)
  waiting for transfers between devices  20.4 us (22%)
  starting transfers between devices  16.2 us (18%)
  local copies, waits for them, and re-layouts  7.14 us (8%)
  other arithmetic  3.56 us (4%)
    pallas_call x4, Pallas kernels, attend(): pl.pallas_call(attend_kernel, grid=(n,), in_specs=in_specs, out_specs=wid...  42.8 us
    ppermute x4, waiting for transfers between devices, layer(): second = lax.ppermute(chunk, AXES, ahead)  19.1 us
    ppermute x4, starting transfers between devices, layer(): second = lax.ppermute(chunk, AXES, ahead)  14 us
    slice x5, local copies, waits for them, and re-layouts, layer(): sent.append(jnp.concatenate([keys[:, cols], values[:, cols]], axis=1))  3.97 us
    select_n x4, other arithmetic, layer(): first = lax.ppermute(jnp.where(even, chunk, second), AXES, swap)  2.52 us
    unnamed x18, local copies, waits for them, and re-layouts  2.31 us
    ppermute x4, starting transfers between devices, layer(): first = lax.ppermute(jnp.where(even, chunk, second), AXES, swap)  2.26 us
  transfers between devices with their start and end apart: 8, of which 3 were waited for; matrix products, arithmetic and copies ran while one was open for 3% of the time, Pallas kernels for 41%

profile of v2, /device:TPU:15, one launch (start us, length us, event | category | flops | bytes accessed | tf_op | source)
XLA Modules:
  0.0 90.3 jit_solution(15663567156655575232)
XLA Ops:
  0.0 1.0 %slice.30 = bf16[512,384]{1,0:T(8,128)(2,1)S(1)} slice(bf16[512,1024]{1,0:T(8,128)(2,1)} %k0.7), slice={[0:512], [0:384]} | slice | bytes 786432 | tf_op jit(solution)/shard_map/slice | solution.py:122
  1.0 1.0 %slice.31 = bf16[512,384]{1,0:T(8,128)(2,1)S(1)} slice(bf16[512,1024]{1,0:T(8,128)(2,1)} %v0.7), slice={[0:512], [0:384]} | slice | bytes 786432 | tf_op jit(solution)/shard_map/slice | solution.py:122
  2.1 0.9 %pad_maximum_fusion = bf16[512,768]{1,0:T(8,128)(2,1)} fusion(bf16[512,384]{1,0:T(8,128)(2,1)S(1)} %slice.31, bf16[512,384]{1,0:T(8,128)(2,1)S(1)} %slice.30), kind=kLoop, calls=%fused_computation | loop fusion | flops 1572864 | bytes 1572864 | tf_op jit(solution)/shard_map/concatenate | solution.py:122
  3.0 0.0 copy-start
  3.0 0.0 copy-start.1
  3.0 3.2 %collective-permute-start.3 = (bf16[512,768]{1,0:T(8,128)(2,1)}, bf16[512,768]{1,0:T(8,128)(2,1)}, u32[]{:S(2)}, u32[]{:S(2)}) collective-permute-start(bf16[512,768]{1,0:T(8,128)(2,1)} %pad_maximum_fusion), channel_id=1, source_target_pairs={{0,2},{1,3},{2,4},{3,5},{4,6},{5,7},{6,8},{7,9},{8,10},{9,11},{10,... | collective-permute-start | bytes 2359304 | tf_op jit(solution)/shard_map/ppermute | solution.py:127
  6.3 17.5 %collective-permute-done.3.k2.v2 = bf16[512,768]{1,0:T(8,128)(2,1)} collective-permute-done((bf16[512,768]{1,0:T(8,128)(2,1)}, bf16[512,768]{1,0:T(8,128)(2,1)}, u32[]{:S(2)}, u32[]{:S(2)}) %collective-permute-start.3) | collective-permute-done | bytes 786464 | tf_op jit(solution)/shard_map/ppermute | solution.py:127
  23.8 2.2 %broadcast_select_fusion = bf16[512,768]{1,0:T(8,128)(2,1)} fusion(bf16[512,768]{1,0:T(8,128)(2,1)} %collective-permute-done.3.k2.v2, pred[]{:T(512)S(6)} %eq.5, bf16[512,384]{1,0:T(8,128)(2,1)S(1)} %slice.31, bf16[512,384]{1,0:T(8,128)(2,1)S(1)} %slice.30), kind=kLoop, calls=%fused_computation.1 | loop fusion | flops 1966080 | bytes 2359297 | tf_op jit(solution)/shard_map/jit(_where)/select_n | solution.py:130
  26.0 0.0 copy-start.8
  26.0 0.4 collective-permute-start.4
  26.4 0.0 copy-done
  26.4 0.0 copy-done.1
  26.4 0.1 fusion
  26.5 4.9 %collective-permute-start.2 = (bf16[512,512]{1,0:T(8,128)(2,1)S(1)}, bf16[512,512]{1,0:T(8,128)(2,1)S(1)}, u32[]{:S(2)}, u32[]{:S(2)}) collective-permute-start(bf16[512,512]{1,0:T(8,128)(2,1)S(1)} %pad_maximum_fusion.2), channel_id=1, source_target_pairs={{0,2},{1,3},{2,4},{3,5},{4,6},{5,7},{6,8},{7,9},{8,10},{9,11},{10,... | collective-permute-start | bytes 1572872 | tf_op jit(solution)/shard_map/ppermute | solution.py:127
  31.4 0.0 copy-done.8
  31.4 0.9 copy.11.starts
  32.3 0.0 collective-permute-done.4.k1.v1
  32.3 14.9 %attend.4.rest_0_ = bf16[512,4096]{1,0:T(8,128)(2,1)} custom-call(s32[1]{0:T(128)} %bitcast.place, s32[512,1]{1,0:T(8,128)} %copy.11.starts, bf16[512,4096]{1,0:T(8,128)(2,1)} %q.7, bf16[512,768]{1,0:T(8,128)(2,1)} %collective-permute-done.3.k2.v2, bf16[512,768]{1,0:T(8,128)(2,1)} %collective-permute-done.3.k2.v2, ...), custom_call_target="tpu_custom_call" | custom-call | flops 5435817984 | bytes 5505024 | tf_op jit(solution)/shard_map/attend/pallas_call | solution.py:80
  47.2 0.0 collective-permute-done.2.k2.v2
  47.3 0.0 copy-start.2
  47.3 0.1 broadcast_select_fusion.2
  47.4 0.5 collective-permute-start.5
  47.9 1.9 %collective-permute-start.1 = (bf16[512,512]{1,0:T(8,128)(2,1)S(1)}, bf16[512,512]{1,0:T(8,128)(2,1)S(1)}, u32[]{:S(2)}, u32[]{:S(2)}) collective-permute-start(bf16[512,512]{1,0:T(8,128)(2,1)S(1)} %pad_maximum_fusion.1), channel_id=1, source_target_pairs={{0,2},{1,3},{2,4},{3,5},{4,6},{5,7},{6,8},{7,9},{8,10},{9,11},{10,... | collective-permute-start | bytes 1572872 | tf_op jit(solution)/shard_map/ppermute | solution.py:127
  49.8 0.0 collective-permute-done.5.k1.v1
  49.8 0.0 copy-done.2
  49.8 0.0 copy-start.6
  49.9 0.8 copy-done.6
  50.7 10.9 %attend.5.rest_0_ = bf16[512,4096]{1,0:T(8,128)(2,1)} custom-call(s32[1]{0:T(128)} %bitcast.place, s32[512,1]{1,0:T(8,128)} %copy.11.starts, bf16[512,4096]{1,0:T(8,128)(2,1)} %q.7, bf16[512,512]{1,0:T(8,128)(2,1)} %copy-done.2, bf16[512,512]{1,0:T(8,128)(2,1)} %copy-done.2, bf16[512,512]{1,0:T(8,128)(2,1)} %copy-done.6, ...), custom_call_target="tpu_custom_call", output_to_operand_aliasing={{}: (9, {})} | custom-call | flops 3623878656 | bytes 3670016 | tf_op jit(solution)/shard_map/attend/pallas_call | solution.py:80
  61.5 1.6 %collective-permute-done.1.k2.v2 = bf16[512,512]{1,0:T(8,128)(2,1)S(1)} collective-permute-done((bf16[512,512]{1,0:T(8,128)(2,1)S(1)}, bf16[512,512]{1,0:T(8,128)(2,1)S(1)}, u32[]{:S(2)}, u32[]{:S(2)}) %collective-permute-start.1) | collective-permute-done | bytes 524320 | tf_op jit(solution)/shard_map/ppermute | solution.py:127
  63.2 0.0 copy-start.3
  63.2 0.1 broadcast_select_fusion.1
  63.3 1.0 %collective-permute-start.6 = (bf16[512,512]{1,0:T(8,128)(2,1)S(1)}, bf16[512,512]{1,0:T(8,128)(2,1)S(1)}, u32[]{:S(2)}, u32[]{:S(2)}) collective-permute-start(bf16[512,512]{1,0:T(8,128)(2,1)S(1)} %broadcast_select_fusion.1), channel_id=1, source_target_pairs={{0,1},{1,0},{2,3},{3,2},{4,5},{5,4},{6,7},{7,6},{8,9},{9,8},{10,11... | collective-permute-start | bytes 1572872 | tf_op jit(solution)/shard_map/ppermute | solution.py:130
  64.3 0.9 %slice.24 = bf16[512,128]{1,0:T(8,128)(2,1)S(1)} slice(bf16[512,1024]{1,0:T(8,128)(2,1)} %k0.7), slice={[0:512], [896:1024]} | slice | bytes 262144 | tf_op jit(solution)/shard_map/slice | solution.py:122
  65.2 0.9 %slice.25 = bf16[512,128]{1,0:T(8,128)(2,1)S(1)} slice(bf16[512,1024]{1,0:T(8,128)(2,1)} %v0.7), slice={[0:512], [896:1024]} | slice | bytes 262144 | tf_op jit(solution)/shard_map/slice | solution.py:122
  66.2 3.9 %collective-permute-start = (bf16[512,256]{1,0:T(8,128)(2,1)S(1)}, bf16[512,256]{1,0:T(8,128)(2,1)S(1)}, u32[]{:S(2)}, u32[]{:S(2)}) collective-permute-start(bf16[512,256]{1,0:T(8,128)(2,1)S(1)} %pad_maximum_fusion.3), channel_id=1, source_target_pairs={{0,2},{1,3},{2,4},{3,5},{4,6},{5,7},{6,8},{7,9},{8,10},{9,11},{10,... | collective-permute-start | bytes 786440 | tf_op jit(solution)/shard_map/ppermute | solution.py:127
  70.1 0.0 collective-permute-done.6.k1.v1
  70.1 0.0 copy-done.3
  70.1 0.0 copy-start.5
  70.1 0.8 copy-done.5
  70.9 10.9 %attend.6.rest_0_ = bf16[512,4096]{1,0:T(8,128)(2,1)} custom-call(s32[1]{0:T(128)} %bitcast.place, s32[512,1]{1,0:T(8,128)} %copy.11.starts, bf16[512,4096]{1,0:T(8,128)(2,1)} %q.7, bf16[512,512]{1,0:T(8,128)(2,1)} %copy-done.3, bf16[512,512]{1,0:T(8,128)(2,1)} %copy-done.3, bf16[512,512]{1,0:T(8,128)(2,1)} %copy-done.5, ...), custom_call_target="tpu_custom_call", output_to_operand_aliasing={{}: (9, {})} | custom-call | flops 3623878656 | bytes 3670016 | tf_op jit(solution)/shard_map/attend/pallas_call | solution.py:80
  81.8 0.0 collective-permute-done.k2.v2
  81.8 0.0 copy-start.4
  81.8 0.1 broadcast_select_fusion.3
  81.9 0.4 collective-permute-start.7
  82.3 1.2 %collective-permute-done.7.k1.v1 = bf16[512,256]{1,0:T(8,128)(2,1)S(1)} collective-permute-done((bf16[512,256]{1,0:T(8,128)(2,1)S(1)}, bf16[512,256]{1,0:T(8,128)(2,1)S(1)}, u32[]{:S(2)}, u32[]{:S(2)}) %collective-permute-start.7) | collective-permute-done | bytes 262176 | tf_op jit(solution)/shard_map/ppermute | solution.py:130
  83.5 0.0 copy-done.4
  83.5 0.0 copy-start.7
  83.5 0.7 copy-done.7
  84.2 6.1 %attend.7 = bf16[512,4096]{1,0:T(8,128)(2,1)} custom-call(s32[1]{0:T(128)} %bitcast.place, s32[512,1]{1,0:T(8,128)} %copy.11.starts, bf16[512,4096]{1,0:T(8,128)(2,1)} %q.7, bf16[512,256]{1,0:T(8,128)(2,1)} %copy-done.4, bf16[512,256]{1,0:T(8,128)(2,1)} %copy-done.4, bf16[512,256]{1,0:T(8,128)(2,1)} %copy-done.7, ...), custom_call_target="tpu_custom_call", output_to_operand_aliasing={{}: (9, {})} | custom-call | flops 1811939328 | bytes 1835008 | tf_op jit(solution)/shard_map/attend/pallas_call | solution.py:80
  (3 shorter events, 0.1 us)
Async XLA Ops:
  3.0 23.4 %copy-start = (bf16[512,1024]{1,0:T(8,128)(2,1)S(1)}, bf16[512,1024]{1,0:T(8,128)(2,1)}, u32[]{:S(2)}) copy-start(bf16[512,1024]{1,0:T(8,128)(2,1)} %v0.7) | copy-start | bytes 3145732
  3.0 23.4 %copy-start.1 = (bf16[512,1024]{1,0:T(8,128)(2,1)S(1)}, bf16[512,1024]{1,0:T(8,128)(2,1)}, u32[]{:S(2)}) copy-start(bf16[512,1024]{1,0:T(8,128)(2,1)} %k0.7) | copy-start | bytes 3145732
  3.0 20.8 %collective-permute-start.3 = (bf16[512,768]{1,0:T(8,128)(2,1)}, bf16[512,768]{1,0:T(8,128)(2,1)}, u32[]{:S(2)}, u32[]{:S(2)}) collective-permute-start(bf16[512,768]{1,0:T(8,128)(2,1)} %pad_maximum_fusion), channel_id=1, source_target_pairs={{0,2},{1,3},{2,4},{3,5},{4,6},{5,7},{6,8},{7,9},{8,10},{9,11},{10,... | collective-permute-start | bytes 2359304 | tf_op jit(solution)/shard_map/ppermute | solution.py:127
  26.0 5.5 %copy-start.8 = (s32[512]{0:T(512)S(1)}, s32[512]{0:T(512)}, u32[]{:S(2)}) copy-start(s32[512]{0:T(512)} %param.7) | copy-start | bytes 6148
  26.0 6.3 %collective-permute-start.4 = (bf16[512,768]{1,0:T(8,128)(2,1)}, bf16[512,768]{1,0:T(8,128)(2,1)}, u32[]{:S(2)}, u32[]{:S(2)}) collective-permute-start(bf16[512,768]{1,0:T(8,128)(2,1)} %broadcast_select_fusion), channel_id=1, source_target_pairs={{0,1},{1,0},{2,3},{3,2},{4,5},{5,4},{6,7},{7,6},{8,9},{9,8},{10,11... | collective-permute-start | bytes 2359304 | tf_op jit(solution)/shard_map/ppermute | solution.py:130
  26.5 20.7 %collective-permute-start.2 = (bf16[512,512]{1,0:T(8,128)(2,1)S(1)}, bf16[512,512]{1,0:T(8,128)(2,1)S(1)}, u32[]{:S(2)}, u32[]{:S(2)}) collective-permute-start(bf16[512,512]{1,0:T(8,128)(2,1)S(1)} %pad_maximum_fusion.2), channel_id=1, source_target_pairs={{0,2},{1,3},{2,4},{3,5},{4,6},{5,7},{6,8},{7,9},{8,10},{9,11},{10,... | collective-permute-start | bytes 1572872 | tf_op jit(solution)/shard_map/ppermute | solution.py:127
  47.3 2.6 %copy-start.2 = (bf16[512,512]{1,0:T(8,128)(2,1)}, bf16[512,512]{1,0:T(8,128)(2,1)S(1)}, u32[]{:S(2)}) copy-start(bf16[512,512]{1,0:T(8,128)(2,1)S(1)} %collective-permute-done.2.k2.v2) | copy-start | bytes 1572868
  47.4 2.4 %collective-permute-start.5 = (bf16[512,512]{1,0:T(8,128)(2,1)S(1)}, bf16[512,512]{1,0:T(8,128)(2,1)S(1)}, u32[]{:S(2)}, u32[]{:S(2)}) collective-permute-start(bf16[512,512]{1,0:T(8,128)(2,1)S(1)} %broadcast_select_fusion.2), channel_id=1, source_target_pairs={{0,1},{1,0},{2,3},{3,2},{4,5},{5,4},{6,7},{7,6},{8,9},{9,8},{10,11... | collective-permute-start | bytes 1572872 | tf_op jit(solution)/shard_map/ppermute | solution.py:130
  47.9 15.3 %collective-permute-start.1 = (bf16[512,512]{1,0:T(8,128)(2,1)S(1)}, bf16[512,512]{1,0:T(8,128)(2,1)S(1)}, u32[]{:S(2)}, u32[]{:S(2)}) collective-permute-start(bf16[512,512]{1,0:T(8,128)(2,1)S(1)} %pad_maximum_fusion.1), channel_id=1, source_target_pairs={{0,2},{1,3},{2,4},{3,5},{4,6},{5,7},{6,8},{7,9},{8,10},{9,11},{10,... | collective-permute-start | bytes 1572872 | tf_op jit(solution)/shard_map/ppermute | solution.py:127
  49.8 0.8 copy-start.6
  63.2 7.0 %copy-start.3 = (bf16[512,512]{1,0:T(8,128)(2,1)}, bf16[512,512]{1,0:T(8,128)(2,1)S(1)}, u32[]{:S(2)}) copy-start(bf16[512,512]{1,0:T(8,128)(2,1)S(1)} %collective-permute-done.1.k2.v2) | copy-start | bytes 1572868
  63.3 6.8 %collective-permute-start.6 = (bf16[512,512]{1,0:T(8,128)(2,1)S(1)}, bf16[512,512]{1,0:T(8,128)(2,1)S(1)}, u32[]{:S(2)}, u32[]{:S(2)}) collective-permute-start(bf16[512,512]{1,0:T(8,128)(2,1)S(1)} %broadcast_select_fusion.1), channel_id=1, source_target_pairs={{0,1},{1,0},{2,3},{3,2},{4,5},{5,4},{6,7},{7,6},{8,9},{9,8},{10,11... | collective-permute-start | bytes 1572872 | tf_op jit(solution)/shard_map/ppermute | solution.py:130
  66.2 15.6 %collective-permute-start = (bf16[512,256]{1,0:T(8,128)(2,1)S(1)}, bf16[512,256]{1,0:T(8,128)(2,1)S(1)}, u32[]{:S(2)}, u32[]{:S(2)}) collective-permute-start(bf16[512,256]{1,0:T(8,128)(2,1)S(1)} %pad_maximum_fusion.3), channel_id=1, source_target_pairs={{0,2},{1,3},{2,4},{3,5},{4,6},{5,7},{6,8},{7,9},{8,10},{9,11},{10,... | collective-permute-start | bytes 786440 | tf_op jit(solution)/shard_map/ppermute | solution.py:127
  70.1 0.8 copy-start.5
  81.8 1.7 %copy-start.4 = (bf16[512,256]{1,0:T(8,128)(2,1)}, bf16[512,256]{1,0:T(8,128)(2,1)S(1)}, u32[]{:S(2)}) copy-start(bf16[512,256]{1,0:T(8,128)(2,1)S(1)} %collective-permute-done.k2.v2) | copy-start | bytes 786436
  81.9 1.6 %collective-permute-start.7 = (bf16[512,256]{1,0:T(8,128)(2,1)S(1)}, bf16[512,256]{1,0:T(8,128)(2,1)S(1)}, u32[]{:S(2)}, u32[]{:S(2)}) collective-permute-start(bf16[512,256]{1,0:T(8,128)(2,1)S(1)} %broadcast_select_fusion.3), channel_id=1, source_target_pairs={{0,1},{1,0},{2,3},{3,2},{4,5},{5,4},{6,7},{7,6},{8,9},{9,8},{10,11... | collective-permute-start | bytes 786440 | tf_op jit(solution)/shard_map/ppermute | solution.py:130
  83.5 0.7 copy-start.7

commit v3 on v2

--- a/solution.py
+++ b/solution.py
@@ -96,12 +96,9 @@
 
 
 def chunk_sizes(heads):
-    sizes, left = [], heads
-    while left:
-        n = max(1, -(-left * 3 // 8))
-        sizes.append(n)
-        left -= n
-    return sizes
+    lead = heads // 4
+    half = (heads - lead) // 2
+    return [lead, half, heads - lead - half]
 
 
 def layer(queries, keys, values, doc_start):

time: 90.8 us -> 88 us (0.969)
  the two profiles are of different devices: /device:TPU:15 before, /device:TPU:8 now
where the time goes in v3:
time: 88 us; the launch traced here: 87.4 us
  Pallas kernels  40.5 us (46%)
  waiting for transfers between devices  31.3 us (36%)
  starting transfers between devices  7.59 us (9%)
  local copies, waits for them, and re-layouts  5.65 us (6%)
  other arithmetic  2.24 us (3%)
    pallas_call x3, Pallas kernels, attend(): pl.pallas_call(attend_kernel, grid=(n,), in_specs=in_specs, out_specs=wid...  40.5 us
    ppermute x3, waiting for transfers between devices, layer(): second = lax.ppermute(chunk, AXES, ahead)  29 us
    ppermute x3, starting transfers between devices, layer(): second = lax.ppermute(chunk, AXES, ahead)  7.43 us
    slice x3, local copies, waits for them, and re-layouts, layer(): sent.append(jnp.concatenate([keys[:, cols], values[:, cols]], axis=1))  3.31 us
    ppermute x3, waiting for transfers between devices, layer(): first = lax.ppermute(jnp.where(even, chunk, second), AXES, swap)  2.28 us
  transfers between devices with their start and end apart: 6, of which 4 were waited for; matrix products, arithmetic and copies ran while one was open for 3% of the time, Pallas kernels for 29%

profile of v3, /device:TPU:8, one launch (start us, length us, event | category | flops | bytes accessed | tf_op | source)
XLA Modules:
  0.0 87.4 jit_solution(8285581184163451847)
XLA Ops:
  0.0 0.0 copy-start
  0.0 1.1 %slice.22 = bf16[512,256]{1,0:T(8,128)(2,1)S(1)} slice(bf16[512,1024]{1,0:T(8,128)(2,1)} %k0.5), slice={[0:512], [0:256]} | slice | bytes 524288 | tf_op jit(solution)/shard_map/slice | solution.py:119
  1.1 1.0 %slice.23 = bf16[512,256]{1,0:T(8,128)(2,1)S(1)} slice(bf16[512,1024]{1,0:T(8,128)(2,1)} %v0.5), slice={[0:512], [0:256]} | slice | bytes 524288 | tf_op jit(solution)/shard_map/slice | solution.py:119
  2.0 0.8 pad_maximum_fusion.2
  2.9 3.4 %collective-permute-start.2 = (bf16[512,512]{1,0:T(8,128)(2,1)}, bf16[512,512]{1,0:T(8,128)(2,1)}, u32[]{:S(2)}, u32[]{:S(2)}) collective-permute-start(bf16[512,512]{1,0:T(8,128)(2,1)} %pad_maximum_fusion.2), channel_id=1, source_target_pairs={{0,2},{1,3},{2,4},{3,5},{4,6},{5,7},{6,8},{7,9},{8,10},{9,11},{10,... | collective-permute-start | bytes 1572872 | tf_op jit(solution)/shard_map/ppermute | solution.py:124
  6.3 0.0 copy-done
  6.3 1.3 %fusion = (bf16[512,384]{1,0:T(8,128)(2,1)S(1)}, bf16[512,384]{1,0:T(8,128)(2,1)S(1)}, bf16[512,384]{1,0:T(8,128)(2,1)S(1)}, bf16[512,384]{1,0:T(8,128)(2,1)S(1)}) fusion(bf16[512,1024]{1,0:T(8,128)(2,1)S(1)} %copy-done, bf16[512,1024]{1,0:T(8,128)(2,1)} %v0.5), kind=kLoop, calls=%fused_computation.6 | loop fusion | bytes 3145728 | tf_op jit(solution)/shard_map/slice | solution.py:119
  7.6 0.0 copy-start.3
  7.6 12.9 %collective-permute-done.2.k2.v2 = bf16[512,512]{1,0:T(8,128)(2,1)} collective-permute-done((bf16[512,512]{1,0:T(8,128)(2,1)}, bf16[512,512]{1,0:T(8,128)(2,1)}, u32[]{:S(2)}, u32[]{:S(2)}) %collective-permute-start.2) | collective-permute-done | bytes 524320 | tf_op jit(solution)/shard_map/ppermute | solution.py:124
  20.5 0.9 %broadcast_select_fusion.2 = bf16[512,512]{1,0:T(8,128)(2,1)} fusion(bf16[512,512]{1,0:T(8,128)(2,1)} %collective-permute-done.2.k2.v2, pred[]{:T(512)S(6)} %eq.5, bf16[512,256]{1,0:T(8,128)(2,1)S(1)} %slice.23, bf16[512,256]{1,0:T(8,128)(2,1)S(1)} %slice.22), kind=kLoop, calls=%fused_computation.5 | loop fusion | flops 1310720 | bytes 1572865 | tf_op jit(solution)/shard_map/jit(_where)/select_n | solution.py:127
  21.4 0.0 collective-permute-start.3
  21.5 0.1 pad_maximum_fusion.1
  21.5 1.9 %collective-permute-start.1 = (bf16[512,768]{1,0:T(8,128)(2,1)S(1)}, bf16[512,768]{1,0:T(8,128)(2,1)S(1)}, u32[]{:S(2)}, u32[]{:S(2)}) collective-permute-start(bf16[512,768]{1,0:T(8,128)(2,1)S(1)} %pad_maximum_fusion.1), channel_id=1, source_target_pairs={{0,2},{1,3},{2,4},{3,5},{4,6},{5,7},{6,8},{7,9},{8,10},{9,11},{10,... | collective-permute-start | bytes 2359304 | tf_op jit(solution)/shard_map/ppermute | solution.py:124
  23.5 0.0 copy-done.3
  23.5 0.9 copy.9.starts
  24.3 0.0 collective-permute-done.3.k1.v1
  24.3 10.9 %attend.3.rest_0_ = bf16[512,4096]{1,0:T(8,128)(2,1)} custom-call(s32[1]{0:T(128)} %bitcast.place, s32[512,1]{1,0:T(8,128)} %copy.9.starts, bf16[512,4096]{1,0:T(8,128)(2,1)} %q.5, bf16[512,512]{1,0:T(8,128)(2,1)} %collective-permute-done.2.k2.v2, bf16[512,512]{1,0:T(8,128)(2,1)} %collective-permute-done.2.k2.v2, ...), custom_call_target="tpu_custom_call" | custom-call | flops 3623878656 | bytes 3670016 | tf_op jit(solution)/shard_map/attend/pallas_call | solution.py:80
  35.2 9.9 %collective-permute-done.1.k2.v2 = bf16[512,768]{1,0:T(8,128)(2,1)S(1)} collective-permute-done((bf16[512,768]{1,0:T(8,128)(2,1)S(1)}, bf16[512,768]{1,0:T(8,128)(2,1)S(1)}, u32[]{:S(2)}, u32[]{:S(2)}) %collective-permute-start.1) | collective-permute-done | bytes 786464 | tf_op jit(solution)/shard_map/ppermute | solution.py:124
  45.2 0.0 copy-start.1
  45.2 0.2 broadcast_select_fusion.1
  45.4 0.1 collective-permute-start.4
  45.4 0.1 pad_maximum_fusion
  45.5 0.6 copy-done.1
  46.1 2.1 %collective-permute-start = (bf16[512,768]{1,0:T(8,128)(2,1)S(1)}, bf16[512,768]{1,0:T(8,128)(2,1)S(1)}, u32[]{:S(2)}, u32[]{:S(2)}) collective-permute-start(bf16[512,768]{1,0:T(8,128)(2,1)S(1)} %pad_maximum_fusion), channel_id=1, source_target_pairs={{0,2},{1,3},{2,4},{3,5},{4,6},{5,7},{6,8},{7,9},{8,10},{9,11},{10,... | collective-permute-start | bytes 2359304 | tf_op jit(solution)/shard_map/ppermute | solution.py:124
  48.2 0.0 collective-permute-done.4.k1.v1
  48.2 14.8 %attend.4.rest_0_ = bf16[512,4096]{1,0:T(8,128)(2,1)} custom-call(s32[1]{0:T(128)} %bitcast.place, s32[512,1]{1,0:T(8,128)} %copy.9.starts, bf16[512,4096]{1,0:T(8,128)(2,1)} %q.5, bf16[512,768]{1,0:T(8,128)(2,1)} %copy-done.1, bf16[512,768]{1,0:T(8,128)(2,1)} %copy-done.1, ...), custom_call_target="tpu_custom_call", output_to_operand_aliasing={{}: (9, {})} | custom-call | flops 5435817984 | bytes 5505024 | tf_op jit(solution)/shard_map/attend/pallas_call | solution.py:80
  63.0 6.2 %collective-permute-done.k2.v2 = bf16[512,768]{1,0:T(8,128)(2,1)S(1)} collective-permute-done((bf16[512,768]{1,0:T(8,128)(2,1)S(1)}, bf16[512,768]{1,0:T(8,128)(2,1)S(1)}, u32[]{:S(2)}, u32[]{:S(2)}) %collective-permute-start) | collective-permute-done | bytes 786464 | tf_op jit(solution)/shard_map/ppermute | solution.py:124
  69.1 0.0 copy-start.2
  69.1 0.2 broadcast_select_fusion
  69.3 0.1 collective-permute-start.5
  69.4 2.3 %collective-permute-done.5.k1.v1 = bf16[512,768]{1,0:T(8,128)(2,1)S(1)} collective-permute-done((bf16[512,768]{1,0:T(8,128)(2,1)S(1)}, bf16[512,768]{1,0:T(8,128)(2,1)S(1)}, u32[]{:S(2)}, u32[]{:S(2)}) %collective-permute-start.5) | collective-permute-done | bytes 786464 | tf_op jit(solution)/shard_map/ppermute | solution.py:127
  71.7 0.0 copy-done.2
  71.7 0.0 copy-start.4
  71.7 0.9 %copy-done.4 = bf16[512,768]{1,0:T(8,128)(2,1)} copy-done((bf16[512,768]{1,0:T(8,128)(2,1)}, bf16[512,768]{1,0:T(8,128)(2,1)S(1)}, u32[]{:S(2)}) %copy-start.4) | copy-done | bytes 786456
  72.6 14.8 %attend.5 = bf16[512,4096]{1,0:T(8,128)(2,1)} custom-call(s32[1]{0:T(128)} %bitcast.place, s32[512,1]{1,0:T(8,128)} %copy.9.starts, bf16[512,4096]{1,0:T(8,128)(2,1)} %q.5, bf16[512,768]{1,0:T(8,128)(2,1)} %copy-done.2, bf16[512,768]{1,0:T(8,128)(2,1)} %copy-done.2, bf16[512,768]{1,0:T(8,128)(2,1)} %copy-done.4, ...), custom_call_target="tpu_custom_call", output_to_operand_aliasing={{}: (9, {})} | custom-call | flops 5435817984 | bytes 5505024 | tf_op jit(solution)/shard_map/attend/pallas_call | solution.py:80
Async XLA Ops:
  0.0 6.3 %copy-start = (bf16[512,1024]{1,0:T(8,128)(2,1)S(1)}, bf16[512,1024]{1,0:T(8,128)(2,1)}, u32[]{:S(2)}) copy-start(bf16[512,1024]{1,0:T(8,128)(2,1)} %k0.5) | copy-start | bytes 3145732
  2.9 17.7 %collective-permute-start.2 = (bf16[512,512]{1,0:T(8,128)(2,1)}, bf16[512,512]{1,0:T(8,128)(2,1)}, u32[]{:S(2)}, u32[]{:S(2)}) collective-permute-start(bf16[512,512]{1,0:T(8,128)(2,1)} %pad_maximum_fusion.2), channel_id=1, source_target_pairs={{0,2},{1,3},{2,4},{3,5},{4,6},{5,7},{6,8},{7,9},{8,10},{9,11},{10,... | collective-permute-start | bytes 1572872 | tf_op jit(solution)/shard_map/ppermute | solution.py:124
  7.6 15.9 %copy-start.3 = (s32[512]{0:T(512)S(1)}, s32[512]{0:T(512)}, u32[]{:S(2)}) copy-start(s32[512]{0:T(512)} %param.7) | copy-start | bytes 6148
  21.4 2.9 %collective-permute-start.3 = (bf16[512,512]{1,0:T(8,128)(2,1)}, bf16[512,512]{1,0:T(8,128)(2,1)}, u32[]{:S(2)}, u32[]{:S(2)}) collective-permute-start(bf16[512,512]{1,0:T(8,128)(2,1)} %broadcast_select_fusion.2), channel_id=1, source_target_pairs={{0,1},{1,0},{2,3},{3,2},{4,5},{5,4},{6,7},{7,6},{8,9},{9,8},{10,11... | collective-permute-start | bytes 1572872 | tf_op jit(solution)/shard_map/ppermute | solution.py:127
  21.5 23.6 %collective-permute-start.1 = (bf16[512,768]{1,0:T(8,128)(2,1)S(1)}, bf16[512,768]{1,0:T(8,128)(2,1)S(1)}, u32[]{:S(2)}, u32[]{:S(2)}) collective-permute-start(bf16[512,768]{1,0:T(8,128)(2,1)S(1)} %pad_maximum_fusion.1), channel_id=1, source_target_pairs={{0,2},{1,3},{2,4},{3,5},{4,6},{5,7},{6,8},{7,9},{8,10},{9,11},{10,... | collective-permute-start | bytes 2359304 | tf_op jit(solution)/shard_map/ppermute | solution.py:124
  45.2 0.9 %copy-start.1 = (bf16[512,768]{1,0:T(8,128)(2,1)}, bf16[512,768]{1,0:T(8,128)(2,1)S(1)}, u32[]{:S(2)}) copy-start(bf16[512,768]{1,0:T(8,128)(2,1)S(1)} %collective-permute-done.1.k2.v2) | copy-start | bytes 2359300
  45.4 2.8 %collective-permute-start.4 = (bf16[512,768]{1,0:T(8,128)(2,1)S(1)}, bf16[512,768]{1,0:T(8,128)(2,1)}, u32[]{:S(2)}, u32[]{:S(2)}) collective-permute-start(bf16[512,768]{1,0:T(8,128)(2,1)S(1)} %broadcast_select_fusion.1), channel_id=1, source_target_pairs={{0,1},{1,0},{2,3},{3,2},{4,5},{5,4},{6,7},{7,6},{8,9},{9,8},{10,11... | collective-permute-start | bytes 2359304 | tf_op jit(solution)/shard_map/ppermute | solution.py:127
  46.1 23.1 %collective-permute-start = (bf16[512,768]{1,0:T(8,128)(2,1)S(1)}, bf16[512,768]{1,0:T(8,128)(2,1)S(1)}, u32[]{:S(2)}, u32[]{:S(2)}) collective-permute-start(bf16[512,768]{1,0:T(8,128)(2,1)S(1)} %pad_maximum_fusion), channel_id=1, source_target_pairs={{0,2},{1,3},{2,4},{3,5},{4,6},{5,7},{6,8},{7,9},{8,10},{9,11},{10,... | collective-permute-start | bytes 2359304 | tf_op jit(solution)/shard_map/ppermute | solution.py:124
  69.1 2.5 %copy-start.2 = (bf16[512,768]{1,0:T(8,128)(2,1)}, bf16[512,768]{1,0:T(8,128)(2,1)S(1)}, u32[]{:S(2)}) copy-start(bf16[512,768]{1,0:T(8,128)(2,1)S(1)} %collective-permute-done.k2.v2) | copy-start | bytes 2359300
  69.3 2.4 %collective-permute-start.5 = (bf16[512,768]{1,0:T(8,128)(2,1)S(1)}, bf16[512,768]{1,0:T(8,128)(2,1)S(1)}, u32[]{:S(2)}, u32[]{:S(2)}) collective-permute-start(bf16[512,768]{1,0:T(8,128)(2,1)S(1)} %broadcast_select_fusion), channel_id=1, source_target_pairs={{0,1},{1,0},{2,3},{3,2},{4,5},{5,4},{6,7},{7,6},{8,9},{9,8},{10,11... | collective-permute-start | bytes 2359304 | tf_op jit(solution)/shard_map/ppermute | solution.py:127
  71.7 0.9 %copy-start.4 = (bf16[512,768]{1,0:T(8,128)(2,1)}, bf16[512,768]{1,0:T(8,128)(2,1)S(1)}, u32[]{:S(2)}) copy-start(bf16[512,768]{1,0:T(8,128)(2,1)S(1)} %collective-permute-done.5.k1.v1) | copy-start | bytes 2359300
